TPU v7x, 32 devices: a whole 2x2x4 slice. The times are simulated.
32 devices in a mesh: gx: 8 (over z, y), gy: 4 (over x, core).
Axes of the slice: x: 2, y: 2, z: 4, core: 2. Of those that a mesh axis runs over, the one named last changes fastest.
Arguments:
- start_state: float32 [5, 64, 64, 256], P(None, 'gx', 'gy'), may hold values from -1.5 to 5.5, as said below
- section_state: float32 [5, 64, 64, 256], P(None, 'gx', 'gy'), may hold values from -1.5 to 5.5, as said below
- previous_speed: float32 [], replicated, may hold values from 1.2 to 2.4
Outputs:
- new_state: float32 [5, 64, 64, 256], P(None, 'gx', 'gy')
- next_speed: float32 [], replicated
Inputs may be any that keep to these rules, and one draw needn't show every extreme that they name: `start_state`: density (component 0) lies in 0.7 to 1.3 and the pressure 0.4 (E - |momentum|^2 / (2 density)) in 0.6 to 1.2 in every cell. `section_state`: density (component 0) lies in 0.7 to 1.3 and the pressure 0.4 (E - |momentum|^2 / (2 density)) in 0.6 to 1.2 in every cell.
All inputs are finite; a program needn't handle non-finite values.
Results may differ from a plain program's by a relative error of at most 0.00002.
Values sent between devices are 32-bit elements; how exact they have to be, the bound alone decides.
A program may use at most 64 MiB of HBM per device.

v0:
```python
import functools

import jax
import jax.numpy as jnp
from jax import lax
from jax.experimental import pallas as pl
from jax.experimental.pallas import tpu as pltpu
from jax.sharding import PartitionSpec as P

GAMMA = 1.4
COURANT = 0.3
VISCOSITY = 0.05
CONDUCTION = 0.07
FIRST = (0.8, -0.2, 4.0 / 105.0, -1.0 / 280.0)
SECOND = (1.6, -0.2, 8.0 / 315.0, -1.0 / 560.0)
CENTRE = -205.0 / 72.0
WIDTH = 4
ROWS = 8
MESH = pl.DeviceIdType.MESH


def primitive(q):
    density, m1, m2, m3, energy = q
    inverse = 1.0 / density
    u, v, w = m1 * inverse, m2 * inverse, m3 * inverse
    kinetic = 0.5 * (u * u + v * v + w * w)
    pressure = (GAMMA - 1.0) * (energy - density * kinetic)
    return inverse, (u, v, w), kinetic, pressure


def wave_speed(q):
    inverse, _, kinetic, pressure = primitive(q)
    return jnp.sqrt(2.0 * kinetic) + jnp.sqrt(GAMMA * (pressure * inverse))


def smooth_terms(primitives):
    inverse, (u, v, w), kinetic, pressure = primitives
    return [
        VISCOSITY * u,
        VISCOSITY * v,
        VISCOSITY * w,
        VISCOSITY * kinetic + CONDUCTION * (pressure * inverse),
    ]


def flux_terms(q, primitives, direction):
    _, velocity, _, pressure = primitives
    speed = velocity[direction]
    flux = [q[1 + direction]]
    for k in range(3):
        term = q[1 + k] * speed
        flux.append(term + pressure if k == direction else term)
    flux.append((q[4] + pressure) * speed)
    return flux


def over_peers(devices, body, carry):
    if devices > 64:
        return lax.fori_loop(1, devices, body, carry)
    for k in range(1, devices):
        carry = body(k, carry)
    return carry


def meeting_rounds(nx, ny):
    rounds, known = [], 1
    while 2 * known < nx:
        rounds.append(("gx", known))
        known *= 2
    known = 0
    while 2 * known < ny:
        rounds.append(("gy", max(known, 1)))
        known = 2 * known if known else 1
    return rounds


def kernel(
    nx, ny, start, section, speed, out, next_speed,
    old, sec, acc, fx, fy, sm, xhalo, ylo, yhi, top, got,
    load_sem, xs_sem, xr_sem, ys_sem, yr_sem, ts_sem, tr_sem, meet_sem,
):
    _, cx, cy, nz = old.shape
    tiles = cy // ROWS
    devices = nx * ny
    me_x, me_y = lax.axis_index("gx"), lax.axis_index("gy")
    odd = lax.rem(me_x, 2)

    def on_x(k):
        return (lax.rem(me_x + k, nx), me_y)

    def on_y(k):
        return (me_x, lax.rem(me_y + k, ny))

    neighbours = (on_x(1), on_x(nx - 1), on_y(1), on_y(ny - 1))
    barrier = pltpu.get_barrier_semaphore()
    for device in neighbours:
        pl.semaphore_signal(barrier, inc=1, device_id=device, device_id_type=MESH)
    load_section = pltpu.make_async_copy(section, sec, load_sem.at[0])
    load_start = pltpu.make_async_copy(start, old, load_sem.at[1])
    load_start.start()
    load_section.start()

    def x_copy(turn, t):
        side = 1 - odd if turn == 0 else odd
        first = (1 - side) * (cx - WIDTH)
        return pltpu.make_async_remote_copy(
            src_ref=old.at[:, pl.ds(first, WIDTH), pl.ds(t * ROWS, ROWS), :],
            dst_ref=xhalo.at[side, t],
            send_sem=xs_sem.at[side, t],
            recv_sem=xr_sem.at[side, t],
            device_id=on_x(nx + 1 - 2 * side),
            device_id_type=MESH,
        )

    def x_arrival(turn, t):
        side = odd if turn == 0 else 1 - odd
        return side, pltpu.make_async_remote_copy(
            src_ref=old.at[:, pl.ds(0, WIDTH), pl.ds(t * ROWS, ROWS), :],
            dst_ref=xhalo.at[side, t],
            send_sem=xs_sem.at[side, t],
            recv_sem=xr_sem.at[side, t],
            device_id=on_x(1),
            device_id_type=MESH,
        )

    def y_copy(side):
        rows = pl.ds(cy - ROWS, ROWS) if side == 0 else pl.ds(0, ROWS)
        return pltpu.make_async_remote_copy(
            src_ref=old.at[:, :, rows, :],
            dst_ref=ylo if side == 0 else yhi,
            send_sem=ys_sem.at[side],
            recv_sem=yr_sem.at[side],
            device_id=on_y(1) if side == 0 else on_y(ny - 1),
            device_id_type=MESH,
        )

    load_start.wait()
    pl.semaphore_wait(barrier, 4)
    for turn in range(2):
        for t in range(tiles):
            x_copy(turn, t).start()
        if turn == 0:
            for side in range(2):
                y_copy(side).start()

    rounds = meeting_rounds(nx, ny)

    def meet(r):
        axis, distance = rounds[r]
        for k in (distance, -distance):
            device = on_x(nx + k) if axis == "gx" else on_y(ny + k)
            pl.semaphore_signal(meet_sem.at[r], inc=1, device_id=device, device_id_type=MESH)

    def met(r):
        pl.semaphore_wait(meet_sem.at[r], 2)
        if r + 1 < len(rounds):
            meet(r + 1)

    meet(0)

    scale = 0.25 * (COURANT / speed[0, 0])

    edge = jnp.zeros((WIDTH, cy, nz), jnp.float32)
    for c in range(5):
        fx[c, 0:WIDTH] = edge
        fx[c, cx + WIDTH : cx + 2 * WIDTH] = edge
    for c in range(4):
        sm[c, 0:WIDTH, ROWS : ROWS + cy] = edge
        sm[c, cx + WIDTH : cx + 2 * WIDTH, ROWS : ROWS + cy] = edge

    load_section.wait()

    def along_z(i, _):
        q = [sec[c, i] for c in range(5)]
        prim = primitive(q)
        smooth = smooth_terms(prim)
        for c, term in enumerate(flux_terms(q, prim, 0)):
            fx[c, i + WIDTH] = term
        for c, term in enumerate(flux_terms(q, prim, 1)):
            fy[c, i, ROWS : ROWS + cy] = term
        for c, term in enumerate(smooth):
            sm[c, i + WIDTH, ROWS : ROWS + cy] = term
        for c, term in enumerate(flux_terms(q, prim, 2)):
            total = None
            for m in range(1, WIDTH + 1):
                f = FIRST[m - 1] * term
                if c > 0:
                    s = SECOND[m - 1] * smooth[c - 1]
                    above, below = s - f, s + f
                else:
                    above, below = -f, f
                pair = pltpu.roll(above, nz - m, 1) + pltpu.roll(below, m, 1)
                total = pair if total is None else total + pair
            if c > 0:
                total = total + (3.0 * CENTRE) * smooth[c - 1]
            acc[c, i] = total
        return 0

    lax.fori_loop(0, cx, along_z, 0)
    met(0)

    def along_x(i, _):
        for c in range(5):
            total = acc[c, i]
            for m in range(1, WIDTH + 1):
                total = total - FIRST[m - 1] * (fx[c, i + WIDTH + m] - fx[c, i + WIDTH - m])
                if c > 0:
                    total = total + SECOND[m - 1] * (
                        sm[c - 1, i + WIDTH + m, ROWS : ROWS + cy]
                        + sm[c - 1, i + WIDTH - m, ROWS : ROWS + cy]
                    )
            acc[c, i] = total
        return 0

    lax.fori_loop(0, cx, along_x, 0)
    met(1)

    y_copy(0).wait_recv()
    y_copy(1).wait_recv()

    def along_y(i, _):
        for halo, first in ((ylo, 0), (yhi, ROWS + cy)):
            q = [halo[c, i] for c in range(5)]
            prim = primitive(q)
            for c, term in enumerate(flux_terms(q, prim, 1)):
                fy[c, i, first : first + ROWS] = term
            for c, term in enumerate(smooth_terms(prim)):
                sm[c, i + WIDTH, first : first + ROWS] = term
        for c in range(5):
            total = acc[c, i]
            for m in range(1, WIDTH + 1):
                above, below = ROWS + m, ROWS - m
                total = total - FIRST[m - 1] * (
                    fy[c, i, above : above + cy] - fy[c, i, below : below + cy]
                )
                if c > 0:
                    total = total + SECOND[m - 1] * (
                        sm[c - 1, i + WIDTH, above : above + cy]
                        + sm[c - 1, i + WIDTH, below : below + cy]
                    )
            acc[c, i] = total
        return 0

    lax.fori_loop(0, cx, along_y, 0)
    met(2)
    for r in range(3, len(rounds)):
        met(r)

    largest = None
    for turn in range(2):
        for t in range(tiles):
            rows = slice(t * ROWS, (t + 1) * ROWS)
            side, arrival = x_arrival(turn, t)
            arrival.wait_recv()
            sign = (1 - 2 * side).astype(jnp.float32)
            inner = [side * (cx - 1 - 2 * i) + i for i in range(WIDTH)]
            totals = [[acc[c, inner[i], rows] for c in range(5)] for i in range(WIDTH)]
            for h in range(WIDTH):
                q = [xhalo[side, t, c, side * (WIDTH - 1 - 2 * h) + h] for c in range(5)]
                prim = primitive(q)
                flux = [sign * f for f in flux_terms(q, prim, 0)]
                smooth = smooth_terms(prim)
                for i in range(h + 1):
                    m = i + WIDTH - h
                    for c in range(5):
                        term = FIRST[m - 1] * flux[c]
                        if c > 0:
                            term = term + SECOND[m - 1] * smooth[c - 1]
                        totals[i][c] = totals[i][c] + term
            for i in range(WIDTH):
                new = []
                for c in range(5):
                    value = (
                        0.75 * old[c, inner[i], rows]
                        + 0.25 * sec[c, inner[i], rows]
                        + scale * totals[i][c]
                    )
                    out[c, inner[i], rows] = value
                    new.append(value)
                wave = wave_speed(new)
                largest = wave if largest is None else jnp.maximum(largest, wave)

    def top_copy(k):
        return pltpu.make_async_remote_copy(
            src_ref=top,
            dst_ref=got.at[k],
            send_sem=ts_sem.at[k],
            recv_sem=tr_sem.at[k],
            device_id=(lax.rem(me_x + k // ny, nx), lax.rem(me_y + k % ny, ny)),
            device_id_type=MESH,
        )

    folded = largest[:, 0:128]
    for first in range(128, nz, 128):
        folded = jnp.maximum(folded, largest[:, first : first + 128])
    peak = jnp.max(folded, axis=0, keepdims=True)
    top[...] = peak

    def send(k, _):
        top_copy(k).start()
        return 0

    over_peers(devices, send, 0)
    for turn in range(2):
        for t in range(tiles):
            x_copy(turn, t).wait_send()
    for side in range(2):
        y_copy(side).wait_send()

    def receive(k, peak):
        top_copy(k).wait_recv()
        return jnp.maximum(peak, got[k])

    peak = over_peers(devices, receive, peak)
    next_speed[...] = jnp.broadcast_to(jnp.max(peak, axis=1, keepdims=True), next_speed.shape)

    def sent(k, _):
        top_copy(k).wait_send()
        return 0

    over_peers(devices, sent, 0)


def local(nx, ny, start_state, section_state, previous_speed):
    comps, cx, cy, nz = section_state.shape
    tiles = cy // ROWS
    f32 = jnp.float32
    dma = pltpu.SemaphoreType.DMA
    new_state, newest = pl.pallas_call(
        functools.partial(kernel, nx, ny),
        out_shape=(
            pltpu.VMEM(section_state.shape, f32),
            pltpu.VMEM((1, 128), f32),
        ),
        in_specs=[
            pl.BlockSpec(memory_space=pl.ANY),
            pl.BlockSpec(memory_space=pl.ANY),
            pl.BlockSpec(memory_space=pltpu.SMEM),
        ],
        out_specs=(
            pl.BlockSpec(memory_space=pltpu.VMEM),
            pl.BlockSpec(memory_space=pltpu.VMEM),
        ),
        scratch_shapes=[
            pltpu.VMEM(section_state.shape, f32),
            pltpu.VMEM(section_state.shape, f32),
            pltpu.VMEM(section_state.shape, f32),
            pltpu.VMEM((comps, cx + 2 * WIDTH, cy, nz), f32),
            pltpu.VMEM((comps, cx, cy + 2 * ROWS, nz), f32),
            pltpu.VMEM((comps - 1, cx + 2 * WIDTH, cy + 2 * ROWS, nz), f32),
            pltpu.VMEM((2, tiles, comps, WIDTH, ROWS, nz), f32),
            pltpu.VMEM((comps, cx, ROWS, nz), f32),
            pltpu.VMEM((comps, cx, ROWS, nz), f32),
            pltpu.VMEM((1, 128), f32),
            pltpu.VMEM((nx * ny, 1, 128), f32),
            dma((2,)),
            dma((2, tiles)),
            dma((2, tiles)),
            dma((2,)),
            dma((2,)),
            dma((nx * ny,)),
            dma((nx * ny,)),
            pltpu.SemaphoreType.REGULAR((len(meeting_rounds(nx, ny)),)),
        ],
        compiler_params=pltpu.CompilerParams(collective_id=0, has_side_effects=True),
        name="section_step",
    )(start_state, section_state, previous_speed.reshape(1, 1))
    return new_state, newest[0, 0]


def solution(mesh):
    nx, ny = mesh.shape["gx"], mesh.shape["gy"]
    in_specs = (P(None, "gx", "gy", None), P(None, "gx", "gy", None), P())
    out_specs = (P(None, "gx", "gy", None), P())
    return jax.shard_map(
        functools.partial(local, nx, ny),
        mesh=mesh,
        in_specs=in_specs,
        out_specs=out_specs,
        check_vma=False,
    )
```

profile of v0, /device:TPU:0, one launch (start us, length us, event | category | flops | bytes accessed | tf_op | source)
XLA Modules:
  0.0 29.4 jit_solution(10467711690551935285)
XLA Ops:
  1.3 26.1 %section_step.1 = (f32[5,8,16,256]{3,2,1,0:T(8,128)S(1)}, f32[1,128]{1,0:T(1,128)S(1)}) custom-call(f32[5,8,16,256]{3,2,1,0:T(8,128)} %start.1, f32[5,8,16,256]{3,2,1,0:T(8,128)} %section.1, f32[1,1]{1,0:T(1,128)} %bitcast.3.speed), custom_call_target="tpu_custom_call" | custom-call | tf_op jit(solution)/shard_map/section_step/pallas_call | solution.py:329
  27.4 0.8 %copy.7 = f32[5,8,16,256]{3,2,1,0:T(8,128)} copy(f32[5,8,16,256]{3,2,1,0:T(8,128)S(1)} %get-tuple-element.6) | data formatting | bytes 1310720
where the time goes:
time: 29.5 us; the launch traced here: 29.4 us
  Pallas kernels  26.1 us (88%)
  between operations  2.45 us (8%)
  local copies, waits for them, and re-layouts  0.84 us (3%)
    pallas_call x1, Pallas kernels, local(): pl.pallas_call(functools.partial(kernel, nx, ny), out_shape=(pltpu.VMEM(s...  26.1 us
    unnamed x1, local copies, waits for them, and re-layouts  0.84 us

commit v1 on v0

--- a/solution.py
+++ b/solution.py
@@ -321,12 +321,24 @@
     over_peers(devices, sent, 0)
 
 
+def finish(state, peak, new_state, next_speed, sem):
+    comps = state.shape[0]
+    copies = [
+        pltpu.make_async_copy(state.at[c], new_state.at[c], sem.at[c]) for c in range(comps)
+    ]
+    copies.append(pltpu.make_async_copy(peak, next_speed, sem.at[comps]))
+    for copy in copies:
+        copy.start()
+    for copy in copies:
+        copy.wait()
+
+
 def local(nx, ny, start_state, section_state, previous_speed):
     comps, cx, cy, nz = section_state.shape
     tiles = cy // ROWS
     f32 = jnp.float32
     dma = pltpu.SemaphoreType.DMA
-    new_state, newest = pl.pallas_call(
+    state, peak = pl.pallas_call(
         functools.partial(kernel, nx, ny),
         out_shape=(
             pltpu.VMEM(section_state.shape, f32),
@@ -365,7 +377,21 @@
         compiler_params=pltpu.CompilerParams(collective_id=0, has_side_effects=True),
         name="section_step",
     )(start_state, section_state, previous_speed.reshape(1, 1))
-    return new_state, newest[0, 0]
+    new_state, next_speed = pl.pallas_call(
+        finish,
+        out_shape=(
+            jax.ShapeDtypeStruct(section_state.shape, f32),
+            jax.ShapeDtypeStruct((1, 128), f32),
+        ),
+        in_specs=[pl.BlockSpec(memory_space=pltpu.VMEM)] * 2,
+        out_specs=(pl.BlockSpec(memory_space=pl.ANY), pl.BlockSpec(memory_space=pl.ANY)),
+        scratch_shapes=[dma((comps + 1,))],
+        name="write_out",
+    )(
+        pltpu.with_memory_space_constraint(state, pltpu.VMEM),
+        pltpu.with_memory_space_constraint(peak, pltpu.VMEM),
+    )
+    return new_state, next_speed[0, 0]
 
 
 def solution(mesh):

time: 29.5 us -> 28.4 us (0.963)
  between operations: 2.45 us -> 1.28 us
  Pallas kernels: 26.1 us -> 27 us
  local copies, waits for them, and re-layouts: 0.84 us -> 0 us
    pallas_call x0 -> x1, Pallas kernels: none -> 0.88 us  [local(): pl.pallas_call(finish, out_shape=(jax.ShapeDtypeStruct(section_state.shap...]
    unnamed x1 -> x0, local copies, waits for them, and re-layouts: 0.84 us -> none
where the time goes in v1:
time: 28.4 us; the launch traced here: 28.3 us
  Pallas kernels  27 us (95%)
  between operations  1.28 us (5%)
    pallas_call x1, Pallas kernels, local(): pl.pallas_call(functools.partial(kernel, nx, ny), out_shape=(pltpu.VMEM(s...  26.1 us
    pallas_call x1, Pallas kernels, local(): pl.pallas_call(finish, out_shape=(jax.ShapeDtypeStruct(section_state.shap...  0.88 us

profile of v1, /device:TPU:0, one launch (start us, length us, event | category | flops | bytes accessed | tf_op | source)
XLA Modules:
  0.0 28.3 jit_solution(12817054826488475260)
XLA Ops:
  1.3 26.1 %section_step.1 = (f32[5,8,16,256]{3,2,1,0:T(8,128)S(1)}, f32[1,128]{1,0:T(1,128)S(1)}) custom-call(f32[5,8,16,256]{3,2,1,0:T(8,128)} %start.1, f32[5,8,16,256]{3,2,1,0:T(8,128)} %section.1, f32[1,1]{1,0:T(1,128)} %bitcast.3.speed), custom_call_target="tpu_custom_call" | custom-call | tf_op jit(solution)/shard_map/section_step/pallas_call | solution.py:341
  27.4 0.9 %write_out.1 = (f32[5,8,16,256]{3,2,1,0:T(8,128)}, f32[1,128]{1,0:T(1,128)}) custom-call(f32[5,8,16,256]{3,2,1,0:T(8,128)S(1)} %get-tuple-element.6.state, f32[1,128]{1,0:T(1,128)S(1)} %get-tuple-element.7.peak), custom_call_target="tpu_custom_call" | custom-call | tf_op jit(solution)/shard_map/write_out/pallas_call | solution.py:380

commit v2 on v1

--- a/solution.py
+++ b/solution.py
@@ -16,6 +16,7 @@
 CENTRE = -205.0 / 72.0
 WIDTH = 4
 ROWS = 8
+DETOUR = 1
 MESH = pl.DeviceIdType.MESH
 
 
@@ -76,8 +77,9 @@
 
 def kernel(
     nx, ny, start, section, speed, out, next_speed,
-    old, sec, acc, fx, fy, sm, xhalo, ylo, yhi, top, got,
-    load_sem, xs_sem, xr_sem, ys_sem, yr_sem, ts_sem, tr_sem, meet_sem,
+    old, sec, acc, fx, fy, sm, xhalo, relay, ylo, yhi, top, got,
+    load_sem, ns_sem, nr_sem, fs_sem, fr_sem, ds_sem, dr_sem, rr_sem, rs_sem,
+    ys_sem, yr_sem, ts_sem, tr_sem, meet_sem, ring_sem,
 ):
     _, cx, cy, nz = old.shape
     tiles = cy // ROWS
@@ -91,36 +93,72 @@
     def on_y(k):
         return (me_x, lax.rem(me_y + k, ny))
 
-    neighbours = (on_x(1), on_x(nx - 1), on_y(1), on_y(ny - 1))
+    first, last = me_x == 0, me_x == nx - 1
+    near, far = on_x(nx + 1 - 2 * odd), on_x(nx - 1 + 2 * odd)
+    beyond = on_x(nx + 2 - 4 * odd)
+    detours = first | ((odd == 1) & (me_x < nx - 1))
+    carries = (me_x == 1) | ((odd == 0) & (me_x < nx - 2))
+
     barrier = pltpu.get_barrier_semaphore()
-    for device in neighbours:
-        pl.semaphore_signal(barrier, inc=1, device_id=device, device_id_type=MESH)
+
+    def greet(device, sem=barrier):
+        pl.semaphore_signal(sem, inc=1, device_id=device, device_id_type=MESH)
+
+    for device in (near, on_y(1), on_y(ny - 1)):
+        greet(device)
+
+    @pl.when(jnp.logical_not(first | last))
+    def _():
+        greet(far)
+
+    @pl.when((odd == 0) & (me_x > 0))
+    def _():
+        greet(on_x(nx - 2))
+
     load_section = pltpu.make_async_copy(section, sec, load_sem.at[0])
     load_start = pltpu.make_async_copy(start, old, load_sem.at[1])
     load_start.start()
     load_section.start()
 
-    def x_copy(turn, t):
-        side = 1 - odd if turn == 0 else odd
-        first = (1 - side) * (cx - WIDTH)
+    direct = old.shape[0] - DETOUR
+
+    def remote(src, dst, send_sem, recv_sem, device):
         return pltpu.make_async_remote_copy(
-            src_ref=old.at[:, pl.ds(first, WIDTH), pl.ds(t * ROWS, ROWS), :],
-            dst_ref=xhalo.at[side, t],
-            send_sem=xs_sem.at[side, t],
-            recv_sem=xr_sem.at[side, t],
-            device_id=on_x(nx + 1 - 2 * side),
+            src_ref=src,
+            dst_ref=dst,
+            send_sem=send_sem,
+            recv_sem=recv_sem,
+            device_id=device,
             device_id_type=MESH,
         )
 
-    def x_arrival(turn, t):
-        side = odd if turn == 0 else 1 - odd
-        return side, pltpu.make_async_remote_copy(
-            src_ref=old.at[:, pl.ds(0, WIDTH), pl.ds(t * ROWS, ROWS), :],
-            dst_ref=xhalo.at[side, t],
-            send_sem=xs_sem.at[side, t],
-            recv_sem=xr_sem.at[side, t],
-            device_id=on_x(1),
-            device_id_type=MESH,
+    def edge_of(side, t, comps):
+        return old.at[comps, pl.ds((1 - side) * (cx - WIDTH), WIDTH), pl.ds(t * ROWS, ROWS), :]
+
+    def near_copy(t, side):
+        every = pl.ds(0, old.shape[0])
+        return remote(edge_of(odd, t, every), xhalo.at[side, t], ns_sem.at[t], nr_sem.at[t], near)
+
+    def far_copy(t, side):
+        some = pl.ds(0, direct)
+        return remote(
+            edge_of(1 - odd, t, some), xhalo.at[side, t, some], fs_sem.at[t], fr_sem.at[t], far
+        )
+
+    def rest_copy(t, side):
+        rest = pl.ds(direct, DETOUR)
+        return remote(
+            edge_of(1 - odd, t, rest), xhalo.at[side, t, rest], ds_sem.at[t], dr_sem.at[t], far
+        )
+
+    def detour_copy(t):
+        rest = pl.ds(direct, DETOUR)
+        return remote(edge_of(1 - odd, t, rest), relay.at[t], ds_sem.at[t], rr_sem.at[t], near)
+
+    def carry_copy(t):
+        rest = pl.ds(direct, DETOUR)
+        return remote(
+            relay.at[t], xhalo.at[odd, t, rest], rs_sem.at[t], dr_sem.at[t], beyond
         )
 
     def y_copy(side):
@@ -134,14 +172,41 @@
             device_id_type=MESH,
         )
 
+    def start_far():
+        for t in range(tiles):
+            far_copy(t, 1 - odd).start()
+
+        @pl.when(jnp.logical_not(detours))
+        def _():
+            for t in range(tiles):
+                rest_copy(t, 1 - odd).start()
+
     load_start.wait()
-    pl.semaphore_wait(barrier, 4)
-    for turn in range(2):
+    carried = jnp.where((odd == 0) & (me_x < nx - 2), 1, 0)
+    pl.semaphore_wait(barrier, jnp.where(first, 3, 4) + carried)
+
+    @pl.when(first)
+    def _():
+        greet(far)
+
+    @pl.when(last)
+    def _():
+        greet(far, ring_sem)
+        greet(on_x(2), ring_sem)
+
+    @pl.when(detours)
+    def _():
         for t in range(tiles):
-            x_copy(turn, t).start()
-        if turn == 0:
-            for side in range(2):
-                y_copy(side).start()
+            detour_copy(t).start()
+
+    @pl.when(jnp.logical_not(first))
+    def _():
+        start_far()
+
+    for t in range(tiles):
+        near_copy(t, odd).start()
+    for side in range(2):
+        y_copy(side).start()
 
     rounds = meeting_rounds(nx, ny)
 
@@ -155,8 +220,6 @@
         pl.semaphore_wait(meet_sem.at[r], 2)
         if r + 1 < len(rounds):
             meet(r + 1)
-
-    meet(0)
 
     scale = 0.25 * (COURANT / speed[0, 0])
 
@@ -197,7 +260,22 @@
         return 0
 
     lax.fori_loop(0, cx, along_z, 0)
-    met(0)
+
+    @pl.when(first | (me_x == 1))
+    def _():
+        pl.semaphore_wait(ring_sem, 1)
+
+    @pl.when(first)
+    def _():
+        start_far()
+
+    @pl.when(carries)
+    def _():
+        for t in range(tiles):
+            detour_copy(t).wait_recv()
+            carry_copy(t).start()
+
+    meet(0)
 
     def along_x(i, _):
         for c in range(5):
@@ -213,6 +291,7 @@
         return 0
 
     lax.fori_loop(0, cx, along_x, 0)
+    met(0)
     met(1)
 
     y_copy(0).wait_recv()
@@ -247,11 +326,16 @@
         met(r)
 
     largest = None
-    for turn in range(2):
-        for t in range(tiles):
+    for t in range(tiles):
+        for turn in range(2):
             rows = slice(t * ROWS, (t + 1) * ROWS)
-            side, arrival = x_arrival(turn, t)
-            arrival.wait_recv()
+            if turn == 0:
+                side = odd
+                far_copy(t, side).wait_recv()
+                rest_copy(t, side).wait_recv()
+            else:
+                side = 1 - odd
+                near_copy(t, side).wait_recv()
             sign = (1 - 2 * side).astype(jnp.float32)
             inner = [side * (cx - 1 - 2 * i) + i for i in range(WIDTH)]
             totals = [[acc[c, inner[i], rows] for c in range(5)] for i in range(WIDTH)]
@@ -301,9 +385,16 @@
         return 0
 
     over_peers(devices, send, 0)
-    for turn in range(2):
+    for t in range(tiles):
+        near_copy(t, odd).wait_send()
+        far_copy(t, 1 - odd).wait_send()
+        rest_copy(t, 1 - odd).wait_send()
+
+    @pl.when(carries)
+    def _():
         for t in range(tiles):
-            x_copy(turn, t).wait_send()
+            carry_copy(t).wait_send()
+
     for side in range(2):
         y_copy(side).wait_send()
 
@@ -361,18 +452,26 @@
             pltpu.VMEM((comps, cx, cy + 2 * ROWS, nz), f32),
             pltpu.VMEM((comps - 1, cx + 2 * WIDTH, cy + 2 * ROWS, nz), f32),
             pltpu.VMEM((2, tiles, comps, WIDTH, ROWS, nz), f32),
+            pltpu.VMEM((tiles, DETOUR, WIDTH, ROWS, nz), f32),
             pltpu.VMEM((comps, cx, ROWS, nz), f32),
             pltpu.VMEM((comps, cx, ROWS, nz), f32),
             pltpu.VMEM((1, 128), f32),
             pltpu.VMEM((nx * ny, 1, 128), f32),
             dma((2,)),
-            dma((2, tiles)),
-            dma((2, tiles)),
+            dma((tiles,)),
+            dma((tiles,)),
+            dma((tiles,)),
+            dma((tiles,)),
+            dma((tiles,)),
+            dma((tiles,)),
+            dma((tiles,)),
+            dma((tiles,)),
             dma((2,)),
             dma((2,)),
             dma((nx * ny,)),
             dma((nx * ny,)),
             pltpu.SemaphoreType.REGULAR((len(meeting_rounds(nx, ny)),)),
+            pltpu.SemaphoreType.REGULAR,
         ],
         compiler_params=pltpu.CompilerParams(collective_id=0, has_side_effects=True),
         name="section_step",

time: 28.4 us -> 27.6 us (0.972)
  Pallas kernels: 27 us -> 26.1 us
    pallas_call x1, Pallas kernels: 26.1 us -> 25.2 us  [local(): pl.pallas_call(functools.partial(kernel, nx, ny), out_shape=(pltpu.VMEM(s...]
where the time goes in v2:
time: 27.6 us; the launch traced here: 27.4 us
  Pallas kernels  26.1 us (95%)
  between operations  1.28 us (5%)
    pallas_call x1, Pallas kernels, local(): pl.pallas_call(functools.partial(kernel, nx, ny), out_shape=(pltpu.VMEM(s...  25.2 us
    pallas_call x1, Pallas kernels, local(): pl.pallas_call(finish, out_shape=(jax.ShapeDtypeStruct(section_state.shap...  0.88 us

profile of v2, /device:TPU:0, one launch (start us, length us, event | category | flops | bytes accessed | tf_op | source)
XLA Modules:
  0.0 27.4 jit_solution(2680450277465156466)
XLA Ops:
  1.3 25.2 %section_step.1 = (f32[5,8,16,256]{3,2,1,0:T(8,128)S(1)}, f32[1,128]{1,0:T(1,128)S(1)}) custom-call(f32[5,8,16,256]{3,2,1,0:T(8,128)} %start.1, f32[5,8,16,256]{3,2,1,0:T(8,128)} %section.1, f32[1,1]{1,0:T(1,128)} %bitcast.3.speed), custom_call_target="tpu_custom_call" | custom-call | tf_op jit(solution)/shard_map/section_step/pallas_call | solution.py:432
  26.5 0.9 %write_out.1 = (f32[5,8,16,256]{3,2,1,0:T(8,128)}, f32[1,128]{1,0:T(1,128)}) custom-call(f32[5,8,16,256]{3,2,1,0:T(8,128)S(1)} %get-tuple-element.6.state, f32[1,128]{1,0:T(1,128)S(1)} %get-tuple-element.7.peak), custom_call_target="tpu_custom_call" | custom-call | tf_op jit(solution)/shard_map/write_out/pallas_call | solution.py:479

commit v3 on v2

--- a/solution.py
+++ b/solution.py
@@ -53,14 +53,6 @@
         flux.append(term + pressure if k == direction else term)
     flux.append((q[4] + pressure) * speed)
     return flux
-
-
-def over_peers(devices, body, carry):
-    if devices > 64:
-        return lax.fori_loop(1, devices, body, carry)
-    for k in range(1, devices):
-        carry = body(k, carry)
-    return carry
 
 
 def meeting_rounds(nx, ny):
@@ -364,15 +356,15 @@
                 wave = wave_speed(new)
                 largest = wave if largest is None else jnp.maximum(largest, wave)
 
+    me = me_x * ny + me_y
+
     def top_copy(k):
-        return pltpu.make_async_remote_copy(
-            src_ref=top,
-            dst_ref=got.at[k],
-            send_sem=ts_sem.at[k],
-            recv_sem=tr_sem.at[k],
-            device_id=(lax.rem(me_x + k // ny, nx), lax.rem(me_y + k % ny, ny)),
-            device_id_type=MESH,
-        )
+        to = k + (k >= me).astype(jnp.int32)
+        return remote(top, got.at[me], ts_sem, tr_sem, (to // ny, lax.rem(to, ny)))
+
+    def every_top():
+        others = pl.ds(0, devices - 1)
+        return remote(got.at[others], got.at[others], ts_sem, tr_sem, near)
 
     folded = largest[:, 0:128]
     for first in range(128, nz, 128):
@@ -384,7 +376,8 @@
         top_copy(k).start()
         return 0
 
-    over_peers(devices, send, 0)
+    lax.fori_loop(0, devices - 1, send, 0, unroll=devices <= 64)
+    got[me] = peak
     for t in range(tiles):
         near_copy(t, odd).wait_send()
         far_copy(t, 1 - odd).wait_send()
@@ -398,18 +391,10 @@
     for side in range(2):
         y_copy(side).wait_send()
 
-    def receive(k, peak):
-        top_copy(k).wait_recv()
-        return jnp.maximum(peak, got[k])
-
-    peak = over_peers(devices, receive, peak)
+    every_top().wait_send()
+    every_top().wait_recv()
+    peak = jnp.max(got[...], axis=0)
     next_speed[...] = jnp.broadcast_to(jnp.max(peak, axis=1, keepdims=True), next_speed.shape)
-
-    def sent(k, _):
-        top_copy(k).wait_send()
-        return 0
-
-    over_peers(devices, sent, 0)
 
 
 def finish(state, peak, new_state, next_speed, sem):
@@ -468,8 +453,8 @@
             dma((tiles,)),
             dma((2,)),
             dma((2,)),
-            dma((nx * ny,)),
-            dma((nx * ny,)),
+            dma,
+            dma,
             pltpu.SemaphoreType.REGULAR((len(meeting_rounds(nx, ny)),)),
             pltpu.SemaphoreType.REGULAR,
         ],

time: 27.6 us -> 26.9 us (0.975)
  Pallas kernels: 26.1 us -> 25.5 us
    pallas_call x1, Pallas kernels: 25.2 us -> 24.6 us  [local(): pl.pallas_call(functools.partial(kernel, nx, ny), out_shape=(pltpu.VMEM(s...]
where the time goes in v3:
time: 26.9 us; the launch traced here: 26.8 us
  Pallas kernels  25.5 us (95%)
  between operations  1.28 us (5%)
    pallas_call x1, Pallas kernels, local(): pl.pallas_call(functools.partial(kernel, nx, ny), out_shape=(pltpu.VMEM(s...  24.6 us
    pallas_call x1, Pallas kernels, local(): pl.pallas_call(finish, out_shape=(jax.ShapeDtypeStruct(section_state.shap...  0.88 us

profile of v3, /device:TPU:0, one launch (start us, length us, event | category | flops | bytes accessed | tf_op | source)
XLA Modules:
  0.0 26.8 jit_solution(16373409930964511240)
XLA Ops:
  1.3 24.6 %section_step.1 = (f32[5,8,16,256]{3,2,1,0:T(8,128)S(1)}, f32[1,128]{1,0:T(1,128)S(1)}) custom-call(f32[5,8,16,256]{3,2,1,0:T(8,128)} %start.1, f32[5,8,16,256]{3,2,1,0:T(8,128)} %section.1, f32[1,1]{1,0:T(1,128)} %bitcast.3.speed), custom_call_target="tpu_custom_call" | custom-call | tf_op jit(solution)/shard_map/section_step/pallas_call | solution.py:417
  25.9 0.9 %write_out.1 = (f32[5,8,16,256]{3,2,1,0:T(8,128)}, f32[1,128]{1,0:T(1,128)}) custom-call(f32[5,8,16,256]{3,2,1,0:T(8,128)S(1)} %get-tuple-element.6.state, f32[1,128]{1,0:T(1,128)S(1)} %get-tuple-element.7.peak), custom_call_target="tpu_custom_call" | custom-call | tf_op jit(solution)/shard_map/write_out/pallas_call | solution.py:464

commit v4 on v3

--- a/solution.py
+++ b/solution.py
@@ -99,13 +99,9 @@
     for device in (near, on_y(1), on_y(ny - 1)):
         greet(device)
 
-    @pl.when(jnp.logical_not(first | last))
+    @pl.when((odd == 0) & (me_x > 0))
     def _():
         greet(far)
-
-    @pl.when((odd == 0) & (me_x > 0))
-    def _():
-        greet(on_x(nx - 2))
 
     load_section = pltpu.make_async_copy(section, sec, load_sem.at[0])
     load_start = pltpu.make_async_copy(start, old, load_sem.at[1])
@@ -124,17 +120,33 @@
             device_id_type=MESH,
         )
 
-    def edge_of(side, t, comps):
-        return old.at[comps, pl.ds((1 - side) * (cx - WIDTH), WIDTH), pl.ds(t * ROWS, ROWS), :]
-
-    def near_copy(t, side):
+    slabs = [(t, 0, WIDTH) for t in range(tiles - 1)]
+    slabs += [(tiles - 1, 1, WIDTH - 1), (tiles - 1, 0, 1)]
+
+    def layers_of(side, h, count):
+        return pl.ds(h + side * (WIDTH - 2 * h - count), count)
+
+    def edge_of(side, t, comps, h=0, count=WIDTH):
+        layers = layers_of(side, h, count)
+        layers = pl.ds((1 - side) * (cx - WIDTH) + layers.start, count)
+        return old.at[comps, layers, pl.ds(t * ROWS, ROWS), :]
+
+    def near_copy(n, side):
+        t, h, count = slabs[n]
         every = pl.ds(0, old.shape[0])
-        return remote(edge_of(odd, t, every), xhalo.at[side, t], ns_sem.at[t], nr_sem.at[t], near)
-
-    def far_copy(t, side):
+        return remote(
+            edge_of(odd, t, every, h, count),
+            xhalo.at[side, t, every, layers_of(side, h, count)],
+            ns_sem.at[n], nr_sem.at[n], near,
+        )
+
+    def far_copy(n, side):
+        t, h, count = slabs[n]
         some = pl.ds(0, direct)
         return remote(
-            edge_of(1 - odd, t, some), xhalo.at[side, t, some], fs_sem.at[t], fr_sem.at[t], far
+            edge_of(1 - odd, t, some, h, count),
+            xhalo.at[side, t, some, layers_of(side, h, count)],
+            fs_sem.at[n], fr_sem.at[n], far,
         )
 
     def rest_copy(t, side):
@@ -165,8 +177,8 @@
         )
 
     def start_far():
-        for t in range(tiles):
-            far_copy(t, 1 - odd).start()
+        for n in range(len(slabs)):
+            far_copy(n, 1 - odd).start()
 
         @pl.when(jnp.logical_not(detours))
         def _():
@@ -174,16 +186,18 @@
                 rest_copy(t, 1 - odd).start()
 
     load_start.wait()
-    carried = jnp.where((odd == 0) & (me_x < nx - 2), 1, 0)
-    pl.semaphore_wait(barrier, jnp.where(first, 3, 4) + carried)
+    pl.semaphore_wait(barrier, jnp.where(odd == 1, 4, 3))
 
     @pl.when(first)
     def _():
         greet(far)
 
+    @pl.when(odd == 1)
+    def _():
+        greet(far, ring_sem)
+
     @pl.when(last)
     def _():
-        greet(far, ring_sem)
         greet(on_x(2), ring_sem)
 
     @pl.when(detours)
@@ -191,14 +205,19 @@
         for t in range(tiles):
             detour_copy(t).start()
 
-    @pl.when(jnp.logical_not(first))
+    @pl.when(odd == 1)
     def _():
         start_far()
 
-    for t in range(tiles):
-        near_copy(t, odd).start()
+    for n in range(len(slabs)):
+        near_copy(n, odd).start()
     for side in range(2):
         y_copy(side).start()
+
+    @pl.when((odd == 0) & (me_x > 0))
+    def _():
+        pl.semaphore_wait(ring_sem, 1)
+        start_far()
 
     rounds = meeting_rounds(nx, ny)
 
@@ -318,20 +337,23 @@
         met(r)
 
     largest = None
-    for t in range(tiles):
+    for n, (t, first_h, count) in enumerate(slabs):
+        ends = n + 1 == len(slabs) or slabs[n + 1][0] != t
+        rows = slice(t * ROWS, (t + 1) * ROWS)
         for turn in range(2):
-            rows = slice(t * ROWS, (t + 1) * ROWS)
             if turn == 0:
                 side = odd
-                far_copy(t, side).wait_recv()
-                rest_copy(t, side).wait_recv()
+                far_copy(n, side).wait_recv()
+                if first_h + count == WIDTH:
+                    rest_copy(t, side).wait_recv()
             else:
                 side = 1 - odd
-                near_copy(t, side).wait_recv()
+                near_copy(n, side).wait_recv()
             sign = (1 - 2 * side).astype(jnp.float32)
             inner = [side * (cx - 1 - 2 * i) + i for i in range(WIDTH)]
-            totals = [[acc[c, inner[i], rows] for c in range(5)] for i in range(WIDTH)]
-            for h in range(WIDTH):
+            touched = range(first_h + count)
+            totals = [[acc[c, inner[i], rows] for c in range(5)] for i in touched]
+            for h in range(first_h, first_h + count):
                 q = [xhalo[side, t, c, side * (WIDTH - 1 - 2 * h) + h] for c in range(5)]
                 prim = primitive(q)
                 flux = [sign * f for f in flux_terms(q, prim, 0)]
@@ -343,7 +365,11 @@
                         if c > 0:
                             term = term + SECOND[m - 1] * smooth[c - 1]
                         totals[i][c] = totals[i][c] + term
-            for i in range(WIDTH):
+            for i in touched:
+                if not ends and i < first_h:
+                    for c in range(5):
+                        acc[c, inner[i], rows] = totals[i][c]
+                    continue
                 new = []
                 for c in range(5):
                     value = (
@@ -378,9 +404,10 @@
 
     lax.fori_loop(0, devices - 1, send, 0, unroll=devices <= 64)
     got[me] = peak
+    for n in range(len(slabs)):
+        near_copy(n, odd).wait_send()
+        far_copy(n, 1 - odd).wait_send()
     for t in range(tiles):
-        near_copy(t, odd).wait_send()
-        far_copy(t, 1 - odd).wait_send()
         rest_copy(t, 1 - odd).wait_send()
 
     @pl.when(carries)
@@ -443,10 +470,10 @@
             pltpu.VMEM((1, 128), f32),
             pltpu.VMEM((nx * ny, 1, 128), f32),
             dma((2,)),
-            dma((tiles,)),
-            dma((tiles,)),
-            dma((tiles,)),
-            dma((tiles,)),
+            dma((tiles + 1,)),
+            dma((tiles + 1,)),
+            dma((tiles + 1,)),
+            dma((tiles + 1,)),
             dma((tiles,)),
             dma((tiles,)),
             dma((tiles,)),

time: 26.9 us -> 26.7 us (level)
  no operation moved by 1% of the time
where the time goes in v4:
time: 26.7 us; the launch traced here: 26.6 us
  Pallas kernels  25.3 us (95%)
  between operations  1.28 us (5%)
    pallas_call x1, Pallas kernels, local(): pl.pallas_call(functools.partial(kernel, nx, ny), out_shape=(pltpu.VMEM(s...  24.4 us
    pallas_call x1, Pallas kernels, local(): pl.pallas_call(finish, out_shape=(jax.ShapeDtypeStruct(section_state.shap...  0.88 us

profile of v4, /device:TPU:0, one launch (start us, length us, event | category | flops | bytes accessed | tf_op | source)
XLA Modules:
  0.0 26.6 jit_solution(4344578344236406133)
XLA Ops:
  1.3 24.4 %section_step.1 = (f32[5,8,16,256]{3,2,1,0:T(8,128)S(1)}, f32[1,128]{1,0:T(1,128)S(1)}) custom-call(f32[5,8,16,256]{3,2,1,0:T(8,128)} %start.1, f32[5,8,16,256]{3,2,1,0:T(8,128)} %section.1, f32[1,1]{1,0:T(1,128)} %bitcast.3.speed), custom_call_target="tpu_custom_call" | custom-call | tf_op jit(solution)/shard_map/section_step/pallas_call | solution.py:444
  25.7 0.9 %write_out.1 = (f32[5,8,16,256]{3,2,1,0:T(8,128)}, f32[1,128]{1,0:T(1,128)}) custom-call(f32[5,8,16,256]{3,2,1,0:T(8,128)S(1)} %get-tuple-element.6.state, f32[1,128]{1,0:T(1,128)S(1)} %get-tuple-element.7.peak), custom_call_target="tpu_custom_call" | custom-call | tf_op jit(solution)/shard_map/write_out/pallas_call | solution.py:491

commit v5 on v4

--- a/solution.py
+++ b/solution.py
@@ -211,13 +211,13 @@
 
     for n in range(len(slabs)):
         near_copy(n, odd).start()
+    @pl.when((odd == 0) & (me_x > 0))
+    def _():
+        pl.semaphore_wait(ring_sem, 1)
+        start_far()
+
     for side in range(2):
         y_copy(side).start()
-
-    @pl.when((odd == 0) & (me_x > 0))
-    def _():
-        pl.semaphore_wait(ring_sem, 1)
-        start_far()
 
     rounds = meeting_rounds(nx, ny)
 
@@ -340,15 +340,20 @@
     for n, (t, first_h, count) in enumerate(slabs):
         ends = n + 1 == len(slabs) or slabs[n + 1][0] != t
         rows = slice(t * ROWS, (t + 1) * ROWS)
+        if count == 1:
+            far_copy(n, odd).wait_recv()
+            near_copy(n, 1 - odd).wait_recv()
         for turn in range(2):
             if turn == 0:
                 side = odd
-                far_copy(n, side).wait_recv()
+                if count > 1:
+                    far_copy(n, side).wait_recv()
                 if first_h + count == WIDTH:
                     rest_copy(t, side).wait_recv()
             else:
                 side = 1 - odd
-                near_copy(n, side).wait_recv()
+                if count > 1:
+                    near_copy(n, side).wait_recv()
             sign = (1 - 2 * side).astype(jnp.float32)
             inner = [side * (cx - 1 - 2 * i) + i for i in range(WIDTH)]
             touched = range(first_h + count)

time: 26.7 us -> 26.8 us (level)
  no operation moved by 1% of the time
where the time goes in v5:
time: 26.8 us; the launch traced here: 26.6 us
  Pallas kernels  25.3 us (94%)
  between operations  1.28 us (5%)
    pallas_call x1, Pallas kernels, local(): pl.pallas_call(functools.partial(kernel, nx, ny), out_shape=(pltpu.VMEM(s...  24.5 us
    pallas_call x1, Pallas kernels, local(): pl.pallas_call(finish, out_shape=(jax.ShapeDtypeStruct(section_state.shap...  0.88 us

profile of v5, /device:TPU:0, one launch (start us, length us, event | category | flops | bytes accessed | tf_op | source)
XLA Modules:
  0.0 26.6 jit_solution(11940899226776201777)
XLA Ops:
  1.3 24.5 %section_step.1 = (f32[5,8,16,256]{3,2,1,0:T(8,128)S(1)}, f32[1,128]{1,0:T(1,128)S(1)}) custom-call(f32[5,8,16,256]{3,2,1,0:T(8,128)} %start.1, f32[5,8,16,256]{3,2,1,0:T(8,128)} %section.1, f32[1,1]{1,0:T(1,128)} %bitcast.3.speed), custom_call_target="tpu_custom_call" | custom-call | tf_op jit(solution)/shard_map/section_step/pallas_call | solution.py:449
  25.7 0.9 %write_out.1 = (f32[5,8,16,256]{3,2,1,0:T(8,128)}, f32[1,128]{1,0:T(1,128)}) custom-call(f32[5,8,16,256]{3,2,1,0:T(8,128)S(1)} %get-tuple-element.6.state, f32[1,128]{1,0:T(1,128)S(1)} %get-tuple-element.7.peak), custom_call_target="tpu_custom_call" | custom-call | tf_op jit(solution)/shard_map/write_out/pallas_call | solution.py:496

commit v6 on v5

--- a/solution.py
+++ b/solution.py
@@ -69,8 +69,8 @@
 
 def kernel(
     nx, ny, start, section, speed, out, next_speed,
-    old, sec, acc, fx, fy, sm, xhalo, relay, ylo, yhi, top, got,
-    load_sem, ns_sem, nr_sem, fs_sem, fr_sem, ds_sem, dr_sem, rr_sem, rs_sem,
+    old, sec, acc, fx, fy, sm, xhalo, relay, aside, ylo, yhi, top, got,
+    load_sem, ns_sem, nr_sem, fs_sem, fr_sem, ds_sem, dr_sem, rr_sem, rs_sem, sides_sem, sider_sem,
     ys_sem, yr_sem, ts_sem, tr_sem, meet_sem, ring_sem,
 ):
     _, cx, cy, nz = old.shape
@@ -88,6 +88,7 @@
     first, last = me_x == 0, me_x == nx - 1
     near, far = on_x(nx + 1 - 2 * odd), on_x(nx - 1 + 2 * odd)
     beyond = on_x(nx + 2 - 4 * odd)
+    sidesteps, steps = me_x == nx // 2, me_x == nx // 2 - 1
     detours = first | ((odd == 1) & (me_x < nx - 1))
     carries = (me_x == 1) | ((odd == 0) & (me_x < nx - 2))
 
@@ -99,9 +100,13 @@
     for device in (near, on_y(1), on_y(ny - 1)):
         greet(device)
 
+    @pl.when((odd == 1) & jnp.logical_not(last))
+    def _():
+        greet(far)
+
     @pl.when((odd == 0) & (me_x > 0))
     def _():
-        greet(far)
+        greet(on_x(nx - 2))
 
     load_section = pltpu.make_async_copy(section, sec, load_sem.at[0])
     load_start = pltpu.make_async_copy(start, old, load_sem.at[1])
@@ -133,12 +138,26 @@
 
     def near_copy(n, side):
         t, h, count = slabs[n]
-        every = pl.ds(0, old.shape[0])
+        every = pl.ds(0, old.shape[0] - (n == 0))
         return remote(
             edge_of(odd, t, every, h, count),
             xhalo.at[side, t, every, layers_of(side, h, count)],
             ns_sem.at[n], nr_sem.at[n], near,
         )
+
+    def near_rest_copy(side):
+        rest = pl.ds(old.shape[0] - 1, 1)
+        return remote(
+            edge_of(odd, 0, rest), xhalo.at[side, 0, rest], sides_sem.at[0], sider_sem.at[0], near
+        )
+
+    def sidestep_copy():
+        rest = pl.ds(old.shape[0] - 1, 1)
+        return remote(edge_of(odd, 0, rest), aside, sides_sem.at[0], sider_sem.at[1], far)
+
+    def step_copy():
+        rest = pl.ds(old.shape[0] - 1, 1)
+        return remote(aside, xhalo.at[0, 0, rest], sides_sem.at[1], sider_sem.at[0], on_x(2))
 
     def far_copy(n, side):
         t, h, count = slabs[n]
@@ -185,39 +204,50 @@
             for t in range(tiles):
                 rest_copy(t, 1 - odd).start()
 
+    told = jnp.where(first | ((odd == 1) & jnp.logical_not(last)), 3, 4)
+    pl.semaphore_wait(barrier, told + jnp.where((odd == 0) & (me_x < nx - 2), 1, 0))
+
+    @pl.when(first)
+    def _():
+        greet(far)
+
+    @pl.when(((odd == 0) & (me_x > 0)) | last)
+    def _():
+        greet(far, ring_sem.at[0])
+
+    @pl.when(last)
+    def _():
+        greet(on_x(2), ring_sem.at[1])
+
     load_start.wait()
-    pl.semaphore_wait(barrier, jnp.where(odd == 1, 4, 3))
-
-    @pl.when(first)
-    def _():
-        greet(far)
-
-    @pl.when(odd == 1)
-    def _():
-        greet(far, ring_sem)
-
-    @pl.when(last)
-    def _():
-        greet(on_x(2), ring_sem)
 
     @pl.when(detours)
     def _():
         for t in range(tiles):
             detour_copy(t).start()
 
-    @pl.when(odd == 1)
-    def _():
-        start_far()
+    @pl.when(sidesteps)
+    def _():
+        sidestep_copy().start()
+
+    @pl.when(jnp.logical_not(sidesteps))
+    def _():
+        near_rest_copy(odd).start()
 
     for n in range(len(slabs)):
         near_copy(n, odd).start()
-    @pl.when((odd == 0) & (me_x > 0))
-    def _():
-        pl.semaphore_wait(ring_sem, 1)
+
+    @pl.when(((odd == 0) & (me_x > 0)) | last)
+    def _():
         start_far()
 
     for side in range(2):
         y_copy(side).start()
+
+    @pl.when((odd == 1) & jnp.logical_not(last))
+    def _():
+        pl.semaphore_wait(ring_sem.at[0], 1)
+        start_far()
 
     rounds = meeting_rounds(nx, ny)
 
@@ -272,13 +302,19 @@
 
     lax.fori_loop(0, cx, along_z, 0)
 
-    @pl.when(first | (me_x == 1))
-    def _():
-        pl.semaphore_wait(ring_sem, 1)
+    @pl.when(me_x == 1)
+    def _():
+        pl.semaphore_wait(ring_sem.at[1], 1)
 
     @pl.when(first)
     def _():
+        pl.semaphore_wait(ring_sem.at[0], 1)
         start_far()
+
+    @pl.when(steps)
+    def _():
+        sidestep_copy().wait_recv()
+        step_copy().start()
 
     @pl.when(carries)
     def _():
@@ -354,6 +390,8 @@
                 side = 1 - odd
                 if count > 1:
                     near_copy(n, side).wait_recv()
+                if n == 0:
+                    near_rest_copy(side).wait_recv()
             sign = (1 - 2 * side).astype(jnp.float32)
             inner = [side * (cx - 1 - 2 * i) + i for i in range(WIDTH)]
             touched = range(first_h + count)
@@ -415,6 +453,12 @@
     for t in range(tiles):
         rest_copy(t, 1 - odd).wait_send()
 
+    near_rest_copy(odd).wait_send()
+
+    @pl.when(steps)
+    def _():
+        step_copy().wait_send()
+
     @pl.when(carries)
     def _():
         for t in range(tiles):
@@ -470,6 +514,7 @@
             pltpu.VMEM((comps - 1, cx + 2 * WIDTH, cy + 2 * ROWS, nz), f32),
             pltpu.VMEM((2, tiles, comps, WIDTH, ROWS, nz), f32),
             pltpu.VMEM((tiles, DETOUR, WIDTH, ROWS, nz), f32),
+            pltpu.VMEM((1, WIDTH, ROWS, nz), f32),
             pltpu.VMEM((comps, cx, ROWS, nz), f32),
             pltpu.VMEM((comps, cx, ROWS, nz), f32),
             pltpu.VMEM((1, 128), f32),
@@ -485,10 +530,12 @@
             dma((tiles,)),
             dma((2,)),
             dma((2,)),
+            dma((2,)),
+            dma((2,)),
             dma,
             dma,
             pltpu.SemaphoreType.REGULAR((len(meeting_rounds(nx, ny)),)),
-            pltpu.SemaphoreType.REGULAR,
+            pltpu.SemaphoreType.REGULAR((2,)),
         ],
         compiler_params=pltpu.CompilerParams(collective_id=0, has_side_effects=True),
         name="section_step",

time: 26.8 us -> 26.7 us (level)
  no operation moved by 1% of the time
where the time goes in v6:
time: 26.7 us; the launch traced here: 26.6 us
  Pallas kernels  25.3 us (95%)
  between operations  1.28 us (5%)
    pallas_call x1, Pallas kernels, local(): pl.pallas_call(functools.partial(kernel, nx, ny), out_shape=(pltpu.VMEM(s...  24.4 us
    pallas_call x1, Pallas kernels, local(): pl.pallas_call(finish, out_shape=(jax.ShapeDtypeStruct(section_state.shap...  0.88 us

profile of v6, /device:TPU:0, one launch (start us, length us, event | category | flops | bytes accessed | tf_op | source)
XLA Modules:
  0.0 26.6 jit_solution(6116821319580752494)
XLA Ops:
  1.3 24.4 %section_step.1 = (f32[5,8,16,256]{3,2,1,0:T(8,128)S(1)}, f32[1,128]{1,0:T(1,128)S(1)}) custom-call(f32[5,8,16,256]{3,2,1,0:T(8,128)} %start.1, f32[5,8,16,256]{3,2,1,0:T(8,128)} %section.1, f32[1,1]{1,0:T(1,128)} %bitcast.3.speed), custom_call_target="tpu_custom_call" | custom-call | tf_op jit(solution)/shard_map/section_step/pallas_call | solution.py:493
  25.7 0.9 %write_out.1 = (f32[5,8,16,256]{3,2,1,0:T(8,128)}, f32[1,128]{1,0:T(1,128)}) custom-call(f32[5,8,16,256]{3,2,1,0:T(8,128)S(1)} %get-tuple-element.6.state, f32[1,128]{1,0:T(1,128)S(1)} %get-tuple-element.7.peak), custom_call_target="tpu_custom_call" | custom-call | tf_op jit(solution)/shard_map/write_out/pallas_call | solution.py:543
